TPU v7x, 512 devices: a 8x2x16 block of a 8x8x16 slice. The times are simulated.
512 devices in a mesh: grp: 2 (over y), ep: 128 (over x, z), tp: 2 (over core).
Axes of the slice: x: 8, y: 2, z: 16, core: 2. Of those that a mesh axis runs over, the one named last changes fastest.
The devices are a block of a 8x8x16 slice.
Arguments:
- queries: bfloat16 [16384, 16, 576], P(('grp', 'ep'), 'tp'), parts along dimension 0, may hold values from -450 to 450
- latent_cache: bfloat16 [768, 512, 576], P(('grp', 'ep'), 'tp'), parts along dimension 0, may hold values from -6 to 6
- residual: bfloat16 [16384, 2048], P(('grp', 'ep')), parts along dimension 0, may hold values from -8 to 8
- token_request: int32 [16384], P(('grp', 'ep')), parts along dimension 0, may hold values from 0 to 2, as said below
- token_visible: int32 [16384], P(('grp', 'ep')), parts along dimension 0, may hold values from 1 to 512, as said below
- value_proj: bfloat16 [16, 512, 128], P('tp', 'ep'), may hold values from -0.25 to 0.25
- out_proj: bfloat16 [2048, 2048], P('tp', 'ep'), may hold values from -0.125 to 0.125
- norm_gain: float32 [2048], replicated, may hold values from 0.1 to 1.9
- router: bfloat16 [2048, 64], replicated, may hold values from -0.0390625 to 0.0390625
- expert_ids: int32 [16384, 6], P(('grp', 'ep')), parts along dimension 0, may hold values from 0 to 63, all different within a row; in each aligned block of 64 rows (0 to 63, 64 to 127, ...) at most 8 rows name the same one
- gate_weight: bfloat16 [128, 2048, 384], P('ep', None, 'tp'), may hold values from -0.125 to 0.125
- up_weight: bfloat16 [128, 2048, 384], P('ep', None, 'tp'), may hold values from -0.125 to 0.125
- down_weight: bfloat16 [128, 384, 2048], P('ep', 'tp'), may hold values from -0.21875 to 0.21875
Outputs:
- hidden: bfloat16 [16384, 2048], P(('grp', 'ep'), 'tp'), parts along dimension 0
- expert_out: bfloat16 [16384, 2048], P(('grp', 'ep'), 'tp'), parts along dimension 0
There are 2 independent parts, one for each index of `grp`. A program takes and returns all parts, laid end to end along the dimension named above; an argument that names none is the same for every part. Nothing has to cross between parts.
Inputs may be any that keep to these rules, and one draw needn't show every extreme that they name: `token_request`: in each ep block, 62 tokens belong to request 0, a prefill span, and each other request has exactly one token; the tokens' order in the block is arbitrary. `token_visible`: the span's tokens read consecutive counts s + 1 to s + 62; 512 is reached in every draw. `expert_ids`: each row names 6 different experts; among the 64 tokens of one ep index no expert is named by more than 8 tokens, and this bound is reached.
All inputs are finite; a program needn't handle non-finite values.
Results may differ from a plain program's by a relative error of at most 0.018.
Values may be sent and summed in bfloat16 or wider, within the bound.
A program may use at most 64 MiB of HBM per device.

v0:
```python
import jax
import jax.numpy as jnp
from jax import lax
from jax.sharding import Mesh
from jax.sharding import PartitionSpec as P

LATENT = 512
VDIM = 128
EXPERTS = 64
TOPK = 6
GROUPS = 2
CAP = 8
PIECES = 128
EP = ("ep_0", "ep_1")
GRP_EP = ("grp", "ep_0", "ep_1")
score_scale = 192.0 ** (-0.5)
epsilon = 1e-06


def from_everyone(value, axis):
    peers = lax.axis_size(axis)
    return lax.all_to_all(
        jnp.broadcast_to(value[None], (peers, *value.shape)), axis, 0, 0, tiled=True
    )


def laid_out(pieces, dim):
    lengths = list(pieces.shape[1:])
    lengths[dim] *= pieces.shape[0]
    return jnp.moveaxis(pieces, 0, dim).reshape(lengths)


def collect(value, axis, dim):
    pieces = from_everyone(value, axis)
    return laid_out(pieces, dim)


def of_everyone(value, axis):
    return from_everyone(value, axis).max(axis=0)


def split_up(value, dim, peers):
    before, after = (value.shape[:dim], value.shape[dim + 1 :])
    return jnp.moveaxis(value.reshape(*before, peers, -1, *after), dim, 0)


def sent_and_summed(value, axis, dim):
    peers = lax.axis_size(axis)
    pieces = lax.all_to_all(split_up(value, dim, peers), axis, 0, 0, tiled=True)
    return jnp.sum(pieces, axis=0)


def sent_together(arrays, axis, dim, along):
    columns = [a.reshape(*a.shape[:along], -1) for a in arrays]
    both = jnp.concatenate(columns, axis=along)
    result, at, outs = (sent_and_summed(both, axis, dim), 0, [])
    for a, column in zip(arrays, columns):
        piece = result[..., at : at + column.shape[along]]
        outs.append(piece.reshape(*piece.shape[:along], *a.shape[along:]))
        at += column.shape[along]
    return tuple(outs)


def stacked_from(value, axes, order):
    pieces = value[None]
    for k in order:
        pieces = lax.all_gather(pieces, axes[k], axis=0, tiled=True)
    carried = [lax.axis_size(axes[k]) for k in reversed(order)]
    pieces = pieces.reshape(*carried, *value.shape)
    turned = sorted(range(len(order)), key=lambda place: order[len(order) - 1 - place])
    return pieces.transpose(*turned, *range(len(order), pieces.ndim)).reshape(-1, *value.shape)


def whole_of(value, axes, order, dim):
    return laid_out(stacked_from(value, axes, order), dim)


def over_copies(value, axis):
    everything = from_everyone(value, axis)
    return jnp.sum(everything, axis=0)


def masked_scores(queries, block_rows, token_request, token_visible, offset):
    per_request = block_rows.shape[1]
    flat_rows = block_rows.reshape(-1, block_rows.shape[2])
    scores = (
        jnp.einsum("thc,kc->thk", queries, flat_rows, preferred_element_type=jnp.float32)
        * score_scale
    )
    column = jnp.arange(flat_rows.shape[0], dtype=jnp.int32)
    owner_id = column // per_request
    position = column % per_request + offset
    allowed = (owner_id[None, :] == token_request[:, None]) & (
        position[None, :] < token_visible[:, None]
    )
    return (jnp.where(allowed[:, None, :], scores, -jnp.inf), flat_rows)


def weighted_rows(scores, row_peak, flat_rows):
    weights = jnp.exp(scores - row_peak[:, :, None]).astype(jnp.bfloat16)
    totals = jnp.sum(weights.astype(jnp.float32), axis=2)
    summed = jnp.einsum(
        "thk,kc->thc", weights, flat_rows[:, :LATENT], preferred_element_type=jnp.float32
    )
    return (summed, totals)


def expert_block(arrived, gate_weight, up_weight, down_weight):
    gate_vals = jnp.einsum("prd,pdf->prf", arrived, gate_weight, preferred_element_type=jnp.float32)
    up_vals = jnp.einsum("prd,pdf->prf", arrived, up_weight, preferred_element_type=jnp.float32)
    activated = (jax.nn.silu(gate_vals) * up_vals).astype(jnp.bfloat16)
    return jnp.einsum(
        "prf,pfd->prd", activated, down_weight, preferred_element_type=jnp.float32
    ).astype(jnp.bfloat16)


def body(
    queries,
    latent_cache,
    residual,
    token_request,
    token_visible,
    value_proj,
    out_proj,
    norm_gain,
    router,
    expert_ids,
    gate_weight,
    up_weight,
    down_weight,
):
    all_heads = collect(queries, "tp", 1)
    offset = lax.axis_index("tp") * latent_cache.shape[1]
    scores, flat_rows = masked_scores(all_heads, latent_cache, token_request, token_visible, offset)
    row_peak = of_everyone(jnp.max(scores, axis=2), "tp")
    part_sum, part_total = weighted_rows(scores, row_peak, flat_rows)
    summed, totals = sent_together((part_sum, part_total), "tp", 1, 2)
    context = (summed / totals[:, :, None]).astype(jnp.bfloat16)
    tokens_here = context.shape[0]
    heads_here = context.shape[1]
    head_values = jnp.einsum(
        "thl,hlv->thv",
        context,
        whole_of(value_proj, EP, (0, 1), 1),
        preferred_element_type=jnp.float32,
    )
    heads_out = head_values.astype(jnp.bfloat16).reshape(tokens_here, heads_here * VDIM)
    attention_part = jnp.dot(
        heads_out, whole_of(out_proj, EP, (0, 1), 1), preferred_element_type=jnp.float32
    )
    attention = over_copies(attention_part, "tp")
    hidden = (residual.astype(jnp.float32) + attention).astype(jnp.bfloat16)
    hidden_wide = hidden.astype(jnp.float32)
    normed = (
        hidden_wide
        * lax.rsqrt(jnp.mean(hidden_wide * hidden_wide, axis=1, keepdims=True) + epsilon)
        * norm_gain
    ).astype(jnp.bfloat16)
    logits = jnp.dot(normed, router, preferred_element_type=jnp.float32)
    gate_share = jax.nn.softmax(jnp.take_along_axis(logits, expert_ids, axis=1), axis=1).astype(
        jnp.bfloat16
    )
    flat_ids = expert_ids.reshape(-1)
    position_id = jnp.arange(flat_ids.shape[0], dtype=jnp.int32)
    earlier = (flat_ids[:, None] == flat_ids[None, :]) & (
        position_id[None, :] < position_id[:, None]
    )
    slot_ids = (flat_ids * CAP + jnp.sum(earlier.astype(jnp.int32), axis=1)).reshape(
        tokens_here, TOPK
    )
    targets = jnp.arange(EXPERTS * CAP, dtype=jnp.int32)
    matches = slot_ids[:, :, None] == targets[None, None, :]
    picker = jnp.any(matches, axis=1).T.astype(jnp.bfloat16)
    model_width = normed.shape[1]
    mixing = jnp.sum(
        jnp.where(matches, gate_share[:, :, None], jnp.zeros((), jnp.bfloat16)), axis=1
    )
    mixing = jnp.broadcast_to(
        mixing.reshape(tokens_here, EXPERTS, 1, CAP), (tokens_here, EXPERTS, GROUPS, CAP)
    ).reshape(tokens_here, PIECES * CAP)
    core_count = lax.axis_size("tp")
    half_width = model_width // core_count
    core_start = lax.axis_index("tp") * half_width
    normed_share = lax.dynamic_slice_in_dim(normed, core_start, half_width, 1)
    outgoing = jnp.dot(picker, normed_share, preferred_element_type=jnp.float32).astype(
        jnp.bfloat16
    )
    outgoing = jnp.broadcast_to(
        outgoing.reshape(EXPERTS, 1, CAP, half_width), (EXPERTS, GROUPS, CAP, half_width)
    ).reshape(PIECES, CAP, half_width)
    arrived_share = lax.all_to_all(outgoing, EP, split_axis=0, concat_axis=1, tiled=True)
    arrived = lax.all_gather(arrived_share, "tp", axis=2, tiled=True)
    partial_out = expert_block(arrived, gate_weight, up_weight, down_weight)
    swapped = lax.all_to_all(partial_out[None], "tp", split_axis=3, concat_axis=0, tiled=True)
    returned = lax.all_to_all(swapped, EP, split_axis=2, concat_axis=1, tiled=True)
    returned = returned.reshape(core_count, PIECES * CAP, half_width)
    routed = jnp.einsum("tk,qkd->td", mixing, returned, preferred_element_type=jnp.float32)
    expert_out = routed.astype(jnp.bfloat16)
    hidden_part = lax.dynamic_slice_in_dim(hidden, core_start, half_width, 1)
    return (hidden_part, expert_out)


def solution(mesh):
    finer = Mesh(
        mesh.devices.reshape(mesh.shape["grp"], 8, 16, mesh.shape["tp"]),
        ("grp", "ep_0", "ep_1", "tp"),
    )
    in_specs = (
        P(GRP_EP, "tp", None),
        P(GRP_EP, "tp", None),
        P(GRP_EP, None),
        P(GRP_EP),
        P(GRP_EP),
        P("tp", EP, None),
        P("tp", EP),
        P(),
        P(),
        P(GRP_EP, None),
        P(EP, None, "tp"),
        P(EP, None, "tp"),
        P(EP, "tp", None),
    )
    out_specs = (P(GRP_EP, "tp"), P(GRP_EP, "tp"))
    return jax.shard_map(body, mesh=finer, in_specs=in_specs, out_specs=out_specs, check_vma=False)
```

profile of v0, /device:TPU:320, one launch (start us, length us, event | category | flops | bytes accessed | tf_op | source)
XLA Modules:
  0.0 692.1 jit_solution(127817837888464356)
XLA Ops:
  7.3 26.9 %all-gather = bf16[64,4,128]{2,1,0:T(4,128)(2,1)S(1)} all-gather(bf16[8,4,128]{2,1,0:T(4,128)(2,1)} %param.18), channel_id=2, replica_groups=mesh['grp'=2,'ep_0'=8,'ep_1'=16,'tp'=2] {'ep_0'}, dimensions={0}, use_global_device_ids=true | all-gather | bytes 73728 | tf_op jit(solution)/shard_map/all_gather | solution.py:67
  34.1 0.6 copy.183
  34.9 25.1 %all-gather.1 = bf16[8192,16]{0,1:T(8,128)(2,1)S(1)} all-gather(bf16[1024,16]{0,1:T(8,128)(2,1)} %param.19), channel_id=3, replica_groups=mesh['grp'=2,'ep_0'=8,'ep_1'=16,'tp'=2] {'ep_0'}, dimensions={0}, use_global_device_ids=true | all-gather | bytes 294912 | tf_op jit(solution)/shard_map/all_gather | solution.py:67
  60.0 0.9 copy.205
  61.0 2.3 broadcast_in_dim.49
  63.2 3.7 all-to-all-start
  66.9 1.5 copy.173
  68.6 0.6 all-to-all-done
  69.1 3.2 fusion.4
  72.5 3.7 all_to_all.59
  76.2 0.5 broadcast.146
  76.7 0.7 reduce.3
  77.5 2.9 convert_reduce_fusion.1
  80.8 3.1 convolution_bitcast_fusion
  83.9 1.8 maximum_bitcast_fusion
  85.6 4.0 all-to-all-start.2
  89.7 0.3 all-gather.10.cloned.1.call-start
  90.7 2.2 all-to-all-done.2
  92.9 1.4 reduce_sum.78
  94.2 1.0 slice.16
  95.2 0.4 copy.198
  95.8 1.4 fusion.16
  97.2 36.4 %all-gather.6.cloned.1.call-done = bf16[128,8,4,128]{3,1,2,0:T(8,128)(2,1)} async-done(((bf16[8,8,4,128]{3,1,2,0:T(8,128)(2,1)}), bf16[128,8,4,128]{3,1,2,0:T(8,128)(2,1)}) %all-gather.6.cloned.1.call-update) | async-done | bytes 1048592 | tf_op jit(solution)/shard_map/all_gather | solution.py:67
  133.6 1.8 copy.184
  135.4 0.4 fusion.15
  135.8 76.6 %all-gather.8.cloned.1.call-done = bf16[128,1024,16]{1,0,2:T(8,128)(2,1)} async-done(((bf16[8,1024,16]{1,0,2:T(8,128)(2,1)}), bf16[128,1024,16]{1,0,2:T(8,128)(2,1)}) %all-gather.8.cloned.1.call-update) | async-done | bytes 4194320 | tf_op jit(solution)/shard_map/all_gather | solution.py:67
  212.5 4.5 copy.188
  217.0 1.4 fusion.36
  218.5 4.6 all_to_all.60
  223.5 0.5 fusion.5
  224.3 118.1 %all_to_all.61 = bf16[128,8,1024]{2,1,0:T(8,128)(2,1)} all-to-all(bf16[128,8,1024]{2,1,0:T(8,128)(2,1)S(1)} %bitcast.107), channel_id=1, replica_groups=mesh['grp'=2,'ep_0'=8,'ep_1'=16,'tp'=2] {'ep_0','ep_1'}, dimensions={0} | all-to-all | bytes 4194304 | tf_op jit(solution)/shard_map/all_to_all | solution.py:191
  342.5 14.4 %all-gather.10.cloned.1.call-done = bf16[1,1024,2048]{2,1,0:T(8,128)(2,1)} async-done(((bf16[1,1024,1024]{2,1,0:T(8,128)(2,1)}), bf16[1,1024,2048]{2,1,0:T(8,128)(2,1)}) %all-gather.10.cloned.1.call-update) | async-done | bytes 4194320 | tf_op jit(solution)/shard_map/all_gather | solution.py:192
  356.9 4.6 fusion.2
  361.5 7.3 %convert_bitcast_fusion = bf16[1,1,1024,2048]{3,2,1,0:T(8,128)(2,1)} fusion(bf16[1,192,2048]{2,1,0:T(8,128)(2,1)S(1)} %copy-done, bf16[1,1024,2048]{2,1,0:T(8,128)(2,1)} %all-gather.10.cloned.1.call-done, bf16[1,2048,192]{1,2,0:T(8,128)(2,1)} %param.24, f32[1024,192]{0,1:T(8,128)} %fusion.2), kind=kOutput, calls=%fused_computation.6 | convolution fusion | flops 1613889536 | bytes 10747904 | tf_op jit(solution)/shard_map/prf,pfd->prd/dot_general | solution.py:112
  368.8 20.6 %copy.194 = bf16[1,1,1024,2048]{2,1,0,3:T(2,128)(2,1)} copy(bf16[1,1,1024,2048]{3,2,1,0:T(8,128)(2,1)} %convert_bitcast_fusion) | data formatting | bytes 8388608 | tf_op jit(solution)/shard_map/broadcast_in_dim | solution.py:194
  389.4 0.5 broadcast.147
  389.9 26.0 %reduce.4 = bf16[2048,1024]{1,0:T(8,128)(2,1)} reduce(bf16[2048,1,1,1024]{3,2,1,0:T(2,128)(2,1)} %bitcast.102, bf16[]{:T(256)} %broadcast.147), dimensions={1,2}, to_apply=%bitcast.85.reduce_sub_computation | reduce | bytes 8388610
  415.9 5.9 reshape.241
  421.8 11.9 %all_to_all.62 = bf16[2,2,524288]{2,1,0:T(2,128)(2,1)} all-to-all(bf16[2,2,524288]{2,1,0:T(2,128)(2,1)} %reshape.241), channel_id=1, replica_groups=mesh['grp'=2,'ep_0'=8,'ep_1'=16,'tp'=2] {'tp'}, dimensions={0} | all-to-all | bytes 8388608 | tf_op jit(solution)/shard_map/all_to_all | solution.py:194
  433.7 7.1 %reshape.242 = bf16[2048,1,1,1024]{3,2,1,0:T(2,128)(2,1)} reshape(bf16[2,2,524288]{2,1,0:T(2,128)(2,1)} %all_to_all.62) | data formatting | bytes 8388608
  440.8 7.1 %copy.200 = bf16[1,1,1024,2048]{2,3,0,1:T(8,128)(2,1)} copy(bf16[1,1,1024,2048]{2,1,0,3:T(2,128)(2,1)} %bitcast.103) | data formatting | bytes 8388608
  447.8 11.3 %copy.195 = bf16[2,1,1024,1024]{3,0,1,2:T(2,128)(2,1)} copy(bf16[2,1,1024,1024]{2,3,0,1:T(8,128)(2,1)} %bitcast.104) | data formatting | bytes 8388608 | tf_op jit(solution)/shard_map/all_to_all | solution.py:194
  459.1 21.4 %all-to-all-start.6 = ((bf16[2,1,1024,1024]{3,0,1,2:T(2,128)(2,1)}), bf16[2,1,1024,1024]{3,0,1,2:T(2,128)(2,1)}, u32[]{:S(2)}, u32[]{:S(2)}) async-start(bf16[2,1,1024,1024]{3,0,1,2:T(2,128)(2,1)} %copy.195), calls=%async_computation.6 | async-start | bytes 8388608 | tf_op jit(solution)/shard_map/all_to_all | solution.py:195
  481.0 2.9 gather_fusion
  484.5 0.7 constant_dynamic-slice_fusion
  485.2 186.6 %all-to-all-done.6 = bf16[2,1,1024,1024]{3,0,1,2:T(2,128)(2,1)} async-done(((bf16[2,1,1024,1024]{3,0,1,2:T(2,128)(2,1)}), bf16[2,1,1024,1024]{3,0,1,2:T(2,128)(2,1)}, u32[]{:S(2)}, u32[]{:S(2)}) %all-to-all-start.6) | async-done | bytes 4194336 | tf_op jit(solution)/shard_map/all_to_all | solution.py:195
  671.8 12.4 %convert_reduce_fusion = bf16[1024,1024]{1,0:T(8,128)(2,1)S(1)} fusion(bf16[2,1,1024,1024]{3,0,1,2:T(2,128)(2,1)} %all-to-all-done.6), kind=kLoop, calls=%fused_computation.1 | loop fusion | flops 3145728 | bytes 6291456 | tf_op jit(solution)/shard_map/tk,qkd->td/reduce_sum | solution.py:197
  684.2 1.2 fusion.55
  (58 shorter events, 3.9 us)
Async XLA Ops:
  7.2 354.3 %copy-start = (bf16[1,192,2048]{2,1,0:T(8,128)(2,1)S(1)}, bf16[1,192,2048]{2,1,0:T(8,128)(2,1)}, u32[]{:S(2)}) copy-start(bf16[1,192,2048]{2,1,0:T(8,128)(2,1)} %param.25) | copy-start | bytes 2359300
  7.2 126.4 %all-gather.6.cloned.1.call-start = ((), (), s32[]{:S(2)}) async-start(), calls=%async_computation.7 | async-start | bytes 1114112 | tf_op jit(solution)/shard_map/all_gather | solution.py:67
  34.8 177.6 %all-gather.8.cloned.1.call-start = ((), (), s32[]{:S(2)}) async-start(), calls=%async_computation.8 | async-start | bytes 4456448 | tf_op jit(solution)/shard_map/all_gather | solution.py:67
  60.9 7.5 %copy-start.6 = (s32[64]{0:T(128)S(1)}, s32[64]{0:T(128)}, u32[]{:S(2)}) copy-start(s32[64]{0:T(128)} %param.17) | copy-start | bytes 772
  60.9 7.5 %copy-start.7 = (s32[64]{0:T(128)S(1)}, s32[64]{0:T(128)}, u32[]{:S(2)}) copy-start(s32[64]{0:T(128)} %param.16) | copy-start | bytes 772
  63.2 5.9 all-to-all-start
  85.6 4.4 copy-start.4
  85.6 7.2 %all-to-all-start.2 = ((f32[2,64,8,513]{3,2,1,0:T(8,128)}), f32[2,64,8,513]{3,2,1,0:T(8,128)S(1)}, u32[]{:S(2)}, u32[]{:S(2)}) async-start(f32[2,64,8,513]{3,2,1,0:T(8,128)} %maximum_bitcast_fusion), calls=%async_computation.2 | async-start | bytes 5242880 | tf_op jit(solution)/shard_map/all_to_all | solution.py:49
  89.7 267.2 %all-gather.10.cloned.1.call-start = ((), (), s32[]{:S(2)}) async-start(), calls=%async_computation.9 | async-start | bytes 6291456 | tf_op jit(solution)/shard_map/all_gather | solution.py:192
  218.4 4.8 copy-start.3
  218.4 5.0 copy-start.5
  224.3 132.6 %copy-start.8 = (bf16[1,2048,192]{1,2,0:T(8,128)(2,1)S(1)}, bf16[1,2048,192]{1,2,0:T(8,128)(2,1)}, u32[]{:S(2)}) copy-start(bf16[1,2048,192]{1,2,0:T(8,128)(2,1)} %param.23) | copy-start | bytes 2359300
  459.1 21.7 %copy-start.2 = (bf16[2048,64]{0,1:T(8,128)(2,1)S(1)}, bf16[2048,64]{0,1:T(8,128)(2,1)}, u32[]{:S(2)}) copy-start(bf16[2048,64]{0,1:T(8,128)(2,1)} %param.21) | copy-start | bytes 786436
  459.1 212.7 %all-to-all-start.6 = ((bf16[2,1,1024,1024]{3,0,1,2:T(2,128)(2,1)}), bf16[2,1,1024,1024]{3,0,1,2:T(2,128)(2,1)}, u32[]{:S(2)}, u32[]{:S(2)}) async-start(bf16[2,1,1024,1024]{3,0,1,2:T(2,128)(2,1)} %copy.195), calls=%async_computation.6 | async-start | bytes 8388608 | tf_op jit(solution)/shard_map/all_to_all | solution.py:195
  484.5 200.9 %copy-start.1 = (bf16[1,192,2048]{2,1,0:T(8,128)(2,1)S(1)}, bf16[1,192,2048]{2,1,0:T(8,128)(2,1)}, u32[]{:S(2)}) copy-start(bf16[1,192,2048]{2,1,0:T(8,128)(2,1)} %param.25) | copy-start | bytes 2359300
Sparse Core Ops, SparseCore 0:
  34.9 98.6 all-gather.5
  135.7 76.7 all-gather.7
  342.6 14.2 all-gather.9
where the time goes:
time: 700 us; the launch traced here: 692 us
  waiting for transfers between devices  317 us (45%)
  blocking collectives  190 us (27%)
  local copies, waits for them, and re-layouts  71.6 us (10%)
  other arithmetic  47.6 us (7%)
  starting transfers between devices  29.5 us (4%)
  matrix products  21.9 us (3%)
  between operations  14.3 us (2%)
    all_to_all x1, waiting for transfers between devices, body(): lax.all_to_all(swapped, EP, split_axis=2, concat_axis=1, tiled=True)  187 us
    all_to_all x1, blocking collectives, body(): lax.all_to_all(outgoing, EP, split_axis=0, concat_axis=1, tiled=True)  118 us
    all_gather x2, waiting for transfers between devices, stacked_from(): pieces = lax.all_gather(pieces, axes[k], axis=0, tiled=True)  113 us
    all_gather x2, blocking collectives, stacked_from(): pieces = lax.all_gather(pieces, axes[k], axis=0, tiled=True)  52 us
    unnamed x1, other arithmetic  26 us
    unnamed x28, local copies, waits for them, and re-layouts  23.3 us
    all_to_all x1, starting transfers between devices, body(): lax.all_to_all(swapped, EP, split_axis=2, concat_axis=1, tiled=True)  21.4 us
    broadcast_in_dim x1, local copies, waits for them, and re-layouts, body(): partial_out[None]  20.6 us
  transfers between devices with their start and end apart: 6, of which 6 were waited for; matrix products, arithmetic and copies ran while one was open for 4% of the time, Pallas kernels for 0%

commit v1 on v0

--- a/solution.py
+++ b/solution.py
@@ -64,7 +64,8 @@
 def stacked_from(value, axes, order):
     pieces = value[None]
     for k in order:
-        pieces = lax.all_gather(pieces, axes[k], axis=0, tiled=True)
+        stack = jnp.stack([pieces] * lax.axis_size(axes[k]))
+        pieces = jnp.concatenate(lax.all_to_all(stack, axes[k], 0, 0), axis=0)
     carried = [lax.axis_size(axes[k]) for k in reversed(order)]
     pieces = pieces.reshape(*carried, *value.shape)
     turned = sorted(range(len(order)), key=lambda place: order[len(order) - 1 - place])

time: 700 us -> 827 us (1.18)
  waiting for transfers between devices: 317 us -> 388 us
  blocking collectives: 190 us -> 246 us
    all_to_all x1 -> x2, waiting for transfers between devices: 2.18 us -> 185 us  [stacked_from(): pieces = jnp.concatenate(lax.all_to_all(stack, axes[k], 0, 0), axis=0)]
    all_gather x2 -> x0, waiting for transfers between devices: 113 us -> none  [stacked_from(): pieces = lax.all_gather(pieces, axes[k], axis=0, tiled=True)]
    all_to_all x0 -> x3, blocking collectives: none -> 108 us  [the longest x2 102 us: stacked_from(): pieces = jnp.concatenate(lax.all_to_all(stack, axes[k], 0, 0), axis=0)]
    all_gather x2 -> x0, blocking collectives: 52 us -> none  [stacked_from(): pieces = lax.all_gather(pieces, axes[k], axis=0, tiled=True)]
    unnamed x28 -> x37, local copies, waits for them, and re-layouts: 23.3 us -> 22.4 us
  transfers between devices with their start and end apart: 6 -> 5, of which waited for: 6 -> 5; matrix products, arithmetic and copies ran while one was open for 4% -> 2% of each run, Pallas kernels for 0% -> 0%
where the time goes in v1:
time: 827 us; the launch traced here: 825 us
  waiting for transfers between devices  388 us (47%)
  blocking collectives  246 us (30%)
  local copies, waits for them, and re-layouts  72.2 us (9%)
  other arithmetic  46.3 us (6%)
  starting transfers between devices  36.7 us (4%)
  matrix products  21.1 us (3%)
  between operations  14.5 us (2%)
    all_to_all x1, waiting for transfers between devices, body(): lax.all_to_all(swapped, EP, split_axis=2, concat_axis=1, tiled=True)  187 us
    all_to_all x2, waiting for transfers between devices, stacked_from(): pieces = jnp.concatenate(lax.all_to_all(stack, axes[k], 0, 0), axis=0)  185 us
    all_to_all x1, blocking collectives, body(): lax.all_to_all(outgoing, EP, split_axis=0, concat_axis=1, tiled=True)  118 us
    all_to_all x2, blocking collectives, stacked_from(): pieces = jnp.concatenate(lax.all_to_all(stack, axes[k], 0, 0), axis=0)  102 us
    unnamed x1, other arithmetic  26 us
    unnamed x37, local copies, waits for them, and re-layouts  22.4 us
    all_to_all x1, starting transfers between devices, body(): lax.all_to_all(swapped, EP, split_axis=2, concat_axis=1, tiled=True)  21.2 us
    broadcast_in_dim x1, local copies, waits for them, and re-layouts, body(): partial_out[None]  20.6 us
  transfers between devices with their start and end apart: 5, of which 5 were waited for; matrix products, arithmetic and copies ran while one was open for 2% of the time, Pallas kernels for 0%

profile of v1, /device:TPU:320, one launch (start us, length us, event | category | flops | bytes accessed | tf_op | source)
XLA Modules:
  0.0 824.6 jit_solution(3625868325850252847)
XLA Ops:
  7.2 2.3 broadcast_in_dim.45
  9.5 3.7 all-to-all-start
  13.2 1.5 copy.139
  14.9 0.6 all-to-all-done
  15.5 3.1 fusion.4
  18.8 3.7 all_to_all.79
  22.5 0.5 broadcast.152
  23.0 0.7 reduce.3
  23.9 3.0 convert_reduce_fusion.1
  26.9 2.4 convolution_bitcast_fusion
  29.9 5.9 all_to_all.80
  35.7 15.5 %all_to_all.81 = bf16[8,1,8,4,128]{4,3,2,1,0:T(4,128)(2,1)S(1)} all-to-all(bf16[8,1,8,4,128]{4,3,2,1,0:T(4,128)(2,1)S(1)} %stack.12), channel_id=1, replica_groups=mesh['grp'=2,'ep_0'=8,'ep_1'=16,'tp'=2] {'ep_0'}, dimensions={0} | all-to-all | bytes 131072 | tf_op jit(solution)/shard_map/all_to_all | solution.py:68
  51.3 0.7 stack.14
  52.0 4.2 all-to-all-start.5
  56.2 10.8 %all-to-all-done.5 = bf16[8,1,1024,16]{2,3,1,0:T(8,128)(2,1)} async-done(((bf16[8,1,1024,16]{2,3,1,0:T(8,128)(2,1)}), bf16[8,1,1024,16]{2,3,1,0:T(8,128)(2,1)}, u32[]{:S(2)}, u32[]{:S(2)}) %all-to-all-start.5) | async-done | bytes 262176 | tf_op jit(solution)/shard_map/all_to_all | solution.py:68
  67.1 0.4 stack.13
  67.5 86.5 %all_to_all.82 = bf16[16,8,8,4,128]{4,3,1,2,0:T(4,128)(2,1)} all-to-all(bf16[16,8,8,4,128]{4,3,1,2,0:T(4,128)(2,1)S(1)} %stack.13), channel_id=1, replica_groups=mesh['grp'=2,'ep_0'=8,'ep_1'=16,'tp'=2] {'ep_1'}, dimensions={0} | all-to-all | bytes 2097152 | tf_op jit(solution)/shard_map/all_to_all | solution.py:68
  154.0 3.4 stack.15
  157.4 7.5 all-to-all-start.6
  165.7 1.5 reduce_sum.78
  167.2 1.1 slice.16
  168.2 0.4 copy.164
  168.9 1.4 fusion.16
  170.3 0.7 copy.150
  170.9 0.4 copy.151
  171.7 174.2 %all-to-all-done.6 = bf16[16,8,1024,16]{2,3,1,0:T(8,128)(2,1)} async-done(((bf16[16,8,1024,16]{2,3,1,0:T(8,128)(2,1)}), bf16[16,8,1024,16]{2,3,1,0:T(8,128)(2,1)}, u32[]{:S(2)}, u32[]{:S(2)}) %all-to-all-start.6) | async-done | bytes 4194336 | tf_op jit(solution)/shard_map/all_to_all | solution.py:68
  346.0 2.6 copy.154
  348.6 1.4 fusion.36
  350.1 4.6 all_to_all.83
  355.2 0.5 fusion.5
  355.9 117.8 %all_to_all.84 = bf16[128,8,1024]{2,1,0:T(8,128)(2,1)} all-to-all(bf16[128,8,1024]{2,1,0:T(8,128)(2,1)S(1)} %bitcast.101), channel_id=1, replica_groups=mesh['grp'=2,'ep_0'=8,'ep_1'=16,'tp'=2] {'ep_0','ep_1'}, dimensions={0} | all-to-all | bytes 4194304 | tf_op jit(solution)/shard_map/all_to_all | solution.py:192
  473.8 15.7 %all-gather.2.cloned.1.call-done = bf16[1,1024,2048]{2,1,0:T(8,128)(2,1)} async-done(((bf16[1,1024,1024]{2,1,0:T(8,128)(2,1)}), bf16[1,1024,2048]{2,1,0:T(8,128)(2,1)}) %all-gather.2.cloned.1.call-update) | async-done | bytes 4194320 | tf_op jit(solution)/shard_map/all_gather | solution.py:193
  489.4 4.6 fusion.2
  494.0 7.3 convert_bitcast_fusion
  501.3 20.6 %copy.160 = bf16[1,1,1024,2048]{2,1,0,3:T(2,128)(2,1)} copy(bf16[1,1,1024,2048]{3,2,1,0:T(8,128)(2,1)} %convert_bitcast_fusion) | data formatting | bytes 8388608 | tf_op jit(solution)/shard_map/broadcast_in_dim | solution.py:195
  521.9 0.5 broadcast.153
  522.4 26.0 %reduce.4 = bf16[2048,1024]{1,0:T(8,128)(2,1)} reduce(bf16[2048,1,1,1024]{3,2,1,0:T(2,128)(2,1)} %bitcast.96, bf16[]{:T(256)} %broadcast.153), dimensions={1,2}, to_apply=%bitcast.79.reduce_sub_computation | reduce | bytes 8388610
  548.4 5.9 reshape.239
  554.3 11.9 %all_to_all.85 = bf16[2,2,524288]{2,1,0:T(2,128)(2,1)} all-to-all(bf16[2,2,524288]{2,1,0:T(2,128)(2,1)} %reshape.239), channel_id=1, replica_groups=mesh['grp'=2,'ep_0'=8,'ep_1'=16,'tp'=2] {'tp'}, dimensions={0} | all-to-all | bytes 8388608 | tf_op jit(solution)/shard_map/all_to_all | solution.py:195
  566.2 7.1 reshape.240
  573.3 7.1 copy.165
  580.3 11.3 %copy.161 = bf16[2,1,1024,1024]{3,0,1,2:T(2,128)(2,1)} copy(bf16[2,1,1024,1024]{2,3,0,1:T(8,128)(2,1)} %bitcast.98) | data formatting | bytes 8388608 | tf_op jit(solution)/shard_map/all_to_all | solution.py:195
  591.7 21.2 %all-to-all-start.10 = ((bf16[2,1,1024,1024]{3,0,1,2:T(2,128)(2,1)}), bf16[2,1,1024,1024]{3,0,1,2:T(2,128)(2,1)}, u32[]{:S(2)}, u32[]{:S(2)}) async-start(bf16[2,1,1024,1024]{3,0,1,2:T(2,128)(2,1)} %copy.161), calls=%async_computation.10 | async-start | bytes 8388608 | tf_op jit(solution)/shard_map/all_to_all | solution.py:196
  613.4 2.9 gather_fusion
  616.9 0.7 constant_dynamic-slice_fusion
  617.5 186.6 %all-to-all-done.10 = bf16[2,1,1024,1024]{3,0,1,2:T(2,128)(2,1)} async-done(((bf16[2,1,1024,1024]{3,0,1,2:T(2,128)(2,1)}), bf16[2,1,1024,1024]{3,0,1,2:T(2,128)(2,1)}, u32[]{:S(2)}, u32[]{:S(2)}) %all-to-all-start.10) | async-done | bytes 4194336 | tf_op jit(solution)/shard_map/all_to_all | solution.py:196
  804.2 12.4 %convert_reduce_fusion = bf16[1024,1024]{1,0:T(8,128)(2,1)S(1)} fusion(bf16[2,1,1024,1024]{3,0,1,2:T(2,128)(2,1)} %all-to-all-done.10), kind=kLoop, calls=%fused_computation.1 | loop fusion | flops 3145728 | bytes 6291456 | tf_op jit(solution)/shard_map/tk,qkd->td/reduce_sum | solution.py:198
  816.6 1.2 fusion.55
  (69 shorter events, 4.3 us)
Async XLA Ops:
  7.2 486.9 %copy-start = (bf16[1,192,2048]{2,1,0:T(8,128)(2,1)S(1)}, bf16[1,192,2048]{2,1,0:T(8,128)(2,1)}, u32[]{:S(2)}) copy-start(bf16[1,192,2048]{2,1,0:T(8,128)(2,1)} %param.25) | copy-start | bytes 2359300
  7.2 7.6 copy-start.11
  7.2 7.6 copy-start.12
  9.5 5.9 all-to-all-start
  14.8 3.9 copy-start.4
  23.9 3.0 copy-start.3
  29.8 5.9 copy-start.10
  29.9 21.4 %copy-start.8 = (bf16[1024,16]{0,1:T(8,128)(2,1)S(1)}, bf16[1024,16]{0,1:T(8,128)(2,1)}, u32[]{:S(2)}) copy-start(bf16[1024,16]{0,1:T(8,128)(2,1)} %param.19) | copy-start | bytes 98308
  52.0 15.1 %all-to-all-start.5 = ((bf16[8,1,1024,16]{2,3,1,0:T(8,128)(2,1)}), bf16[8,1,1024,16]{2,3,1,0:T(8,128)(2,1)}, u32[]{:S(2)}, u32[]{:S(2)}) async-start(bf16[8,1,1024,16]{2,3,1,0:T(8,128)(2,1)} %stack.14), calls=%async_computation.5 | async-start | bytes 524288 | tf_op jit(solution)/shard_map/all_to_all | solution.py:68
  157.4 7.6 copy-start.7
  157.4 188.6 %all-to-all-start.6 = ((bf16[16,8,1024,16]{2,3,1,0:T(8,128)(2,1)}), bf16[16,8,1024,16]{2,3,1,0:T(8,128)(2,1)}, u32[]{:S(2)}, u32[]{:S(2)}) async-start(bf16[16,8,1024,16]{2,3,1,0:T(8,128)(2,1)} %stack.15), calls=%async_computation.6 | async-start | bytes 8388608 | tf_op jit(solution)/shard_map/all_to_all | solution.py:68
  164.9 324.5 %all-gather.2.cloned.1.call-start = ((), (), s32[]{:S(2)}) async-start(), calls=%async_computation.11 | async-start | bytes 6291456 | tf_op jit(solution)/shard_map/all_gather | solution.py:193
  167.2 3.1 copy-start.2
  350.0 4.8 copy-start.6
  350.0 5.0 copy-start.9
  355.9 133.5 %copy-start.13 = (bf16[1,2048,192]{1,2,0:T(8,128)(2,1)S(1)}, bf16[1,2048,192]{1,2,0:T(8,128)(2,1)}, u32[]{:S(2)}) copy-start(bf16[1,2048,192]{1,2,0:T(8,128)(2,1)} %param.23) | copy-start | bytes 2359300
  591.6 21.5 %copy-start.5 = (bf16[2048,64]{0,1:T(8,128)(2,1)S(1)}, bf16[2048,64]{0,1:T(8,128)(2,1)}, u32[]{:S(2)}) copy-start(bf16[2048,64]{0,1:T(8,128)(2,1)} %param.21) | copy-start | bytes 786436
  591.7 212.5 %all-to-all-start.10 = ((bf16[2,1,1024,1024]{3,0,1,2:T(2,128)(2,1)}), bf16[2,1,1024,1024]{3,0,1,2:T(2,128)(2,1)}, u32[]{:S(2)}, u32[]{:S(2)}) async-start(bf16[2,1,1024,1024]{3,0,1,2:T(2,128)(2,1)} %copy.161), calls=%async_computation.10 | async-start | bytes 8388608 | tf_op jit(solution)/shard_map/all_to_all | solution.py:196
  616.9 200.9 %copy-start.1 = (bf16[1,192,2048]{2,1,0:T(8,128)(2,1)S(1)}, bf16[1,192,2048]{2,1,0:T(8,128)(2,1)}, u32[]{:S(2)}) copy-start(bf16[1,192,2048]{2,1,0:T(8,128)(2,1)} %param.25) | copy-start | bytes 2359300
Sparse Core Ops, SparseCore 0:
  473.9 15.4 all-gather.1
